TPU v7x, 32 devices: a whole 2x2x4 slice. The times are simulated.
32 devices in a mesh: grp: 8 (over z, x), sub: 4 (over y, core).
Axes of the slice: x: 2, y: 2, z: 4, core: 2. Of those that a mesh axis runs over, the one named last changes fastest.
Arguments:
- residual: float32 [98304], P(('grp', 'sub')), may hold values from -6 to 6
- edge_scale: float32 [98304], P(('grp', 'sub')), may hold values from 0.2 to 1
- tangent: float32 [3, 98304], P(None, ('grp', 'sub')), may hold values from -6 to 6
- edge_tail: int32 [98304], P(('grp', 'sub')), may hold values from 0 to 511
- edge_head: int32 [98304], P(('grp', 'sub')), may hold values from 0 to 4607
- stencil_index: int32 [14, 16384], P(None, ('grp', 'sub')), may hold values from 0 to 4607
- stencil_coef: bfloat16 [4, 14, 16384], P(None, None, ('grp', 'sub')), may hold values from -1 to -0.099609375
- diag_margin: float32 [4, 16384], P(None, ('grp', 'sub')), may hold values from 0.05 to 0.5
- send_index: int32 [16, 8, 512], P('grp', 'sub'), may hold values from 0 to 511
Outputs:
- correction: float32 [98304], P(('grp', 'sub'))
Inputs may be any that keep to these rules, and one draw needn't show every extreme that they name: `edge_tail`: positions among a device's own nodes. `edge_head`: positions in the device's extended list: own nodes first, then the 8 received blocks. `stencil_index`: positions in the extended list of the device that holds the row. `send_index`: positions among the device's own nodes; an entry may repeat.
All inputs are finite; a program needn't handle non-finite values.
Results may differ from a plain program's by a relative error of at most 0.0003.
Values sent between devices are 32-bit elements; how exact they have to be, the bound alone decides.
A program may use at most 64 MiB of HBM per device.

v0:
```python
import jax
import jax.numpy as jnp
from jax import lax
from jax.sharding import PartitionSpec as P

SWEEPS = 4


def shifted(block, axis, distance):
    devices = range(lax.axis_size(axis))
    route = [((i - distance) % len(devices), i) for i in devices]
    return lax.ppermute(block, axis, route)


def with_halo(value, sides, width):
    for axis, dim in sides:
        devices, length = (lax.axis_size(axis), value.shape[dim])
        up = [(i, (i + 1) % devices) for i in range(devices)]
        down = [(j, i) for i, j in up]
        last = lax.slice_in_dim(value, length - width, length, axis=dim)
        leading = lax.slice_in_dim(value, 0, width, axis=dim)
        before = lax.ppermute(last, axis, up)
        after = lax.ppermute(leading, axis, down)
        value = jnp.concatenate([before, value, after], axis=dim)
    return value


def toward_grp(values, offset):
    return shifted(values, "grp", offset)


def toward_sub(values, offset):
    return shifted(values, "sub", offset)


def ghost_values(owned_vals, send_index):
    blocks = owned_vals[:, send_index]
    widened = with_halo(blocks, (("grp", 1), ("sub", 2)), 1)
    pieces = [widened[:, 0, 1:3], widened[:, 3, 1:3], widened[:, 1:3, 0], widened[:, 1:3, 3]]
    flat_pieces = [piece.reshape(piece.shape[0], -1) for piece in pieces]
    return jnp.concatenate([owned_vals] + flat_pieces, axis=1)


def body(
    residual,
    edge_scale,
    tangent,
    edge_tail,
    edge_head,
    stencil_index,
    stencil_coef,
    diag_margin,
    send_index,
):
    node_count = diag_margin.shape[1]
    rim_size = send_index.shape[2]
    extended = node_count + 8 * rim_size
    half_terms = 0.5 * tangent * residual[None, :]
    vals_tail = jnp.concatenate([-residual[None, :], half_terms], axis=0)
    vals_head = jnp.concatenate([residual[None, :], half_terms], axis=0)
    edge_terms = jnp.zeros((4, extended), jnp.float32)
    edge_terms = edge_terms.at[:, edge_tail].add(vals_tail).at[:, edge_head].add(vals_head)
    node_sums = edge_terms[:, :node_count]
    ghost_terms = edge_terms[:, node_count:].reshape(4, 4, 2, rim_size)
    from_above = toward_grp(ghost_terms[:, 0], -1)
    from_below = toward_grp(ghost_terms[:, 1], 1)
    from_next = toward_sub(ghost_terms[:, 2], -1)
    from_prev = toward_sub(ghost_terms[:, 3], 1)
    node_sums = node_sums.at[:, send_index[1].reshape(-1)].add(from_above.reshape(4, -1))
    node_sums = node_sums.at[:, send_index[0].reshape(-1)].add(from_below.reshape(4, -1))
    node_sums = node_sums.at[:, send_index[:, 1].reshape(-1)].add(from_next.reshape(4, -1))
    node_sums = node_sums.at[:, send_index[:, 0].reshape(-1)].add(from_prev.reshape(4, -1))
    coef_wide = stencil_coef.astype(jnp.float32)
    diag_vals = (1.0 + diag_margin) * jnp.sum(jnp.abs(coef_wide), axis=1)
    solved = node_sums / diag_vals
    for sweep in range(SWEEPS - 1):
        widened = ghost_values(solved, send_index)
        applied = diag_vals * solved + jnp.sum(coef_wide * widened[:, stencil_index], axis=1)
        solved = solved + (node_sums - applied) / diag_vals
    widened = ghost_values(solved, send_index)
    at_tail = widened[:, edge_tail]
    at_head = widened[:, edge_head]
    return (
        edge_scale * residual
        + (at_head[0] - at_tail[0])
        + 0.5 * jnp.sum(tangent * (at_tail[1:] + at_head[1:]), axis=0)
    )


def solution(mesh):
    return jax.shard_map(
        body,
        mesh=mesh,
        in_specs=(
            P(("grp", "sub")),
            P(("grp", "sub")),
            P(None, ("grp", "sub")),
            P(("grp", "sub")),
            P(("grp", "sub")),
            P(None, ("grp", "sub")),
            P(None, None, ("grp", "sub")),
            P(None, ("grp", "sub")),
            P("grp", "sub", None),
        ),
        out_specs=P(("grp", "sub")),
        check_vma=False,
    )
```

profile of v0, /device:TPU:0, one launch (start us, length us, event | category | flops | bytes accessed | tf_op | source)
XLA Modules:
  0.0 282.7 jit_solution(25171760372059289)
XLA Ops:
  2.3 1.7 copy.103
  4.0 1.7 copy.104
  5.7 17.8 %scatter_custom_fusion = f32[4,4608]{0,1:T(8,128)S(1)} fusion(s32[3072]{0:T(1024)S(1)} %get-tuple-element.32, f32[3072,4]{1,0:T(8,128)} %copy.103, f32[]{:T(128)} %constant.6.clone.1), kind=kCustom, calls=%fused_computation.17 | custom fusion | flops 12288 | bytes 74240 | tf_op jit(solution)/shard_map/scatter-add | solution.py:62
  23.5 18.1 %scatter_fusion = f32[4,4608]{0,1:T(8,128)S(1)} fusion(f32[4,4608]{0,1:T(8,128)S(1)} %scatter_custom_fusion, s32[3072]{0:T(1024)S(1)} %get-tuple-element.39, f32[3072,4]{1,0:T(8,128)} %copy.104), kind=kCustom, calls=%fused_computation.10 | custom fusion | flops 12288 | bytes 159744 | tf_op jit(solution)/shard_map/scatter-add | solution.py:62
  43.0 6.0 %collective-permute-start = (f32[4,2,512]{0,2,1:T(8,128)}, f32[4,2,512]{0,2,1:T(8,128)}, u32[]{:S(2)}, u32[]{:S(2)}) collective-permute-start(f32[4,2,512]{0,2,1:T(8,128)} %get-tuple-element.10), channel_id=1, source_target_pairs={{4,0},{8,4},{12,8},{16,12},{20,16},{24,20},{28,24},{0,28},{5,1},{9... | collective-permute-start | bytes 49160 | tf_op jit(solution)/shard_map/ppermute | solution.py:12
  50.0 19.5 %collective-permute-done = f32[4,2,512]{0,2,1:T(8,128)} collective-permute-done((f32[4,2,512]{0,2,1:T(8,128)}, f32[4,2,512]{0,2,1:T(8,128)}, u32[]{:S(2)}, u32[]{:S(2)}) %collective-permute-start) | collective-permute-done | bytes 16416 | tf_op jit(solution)/shard_map/ppermute | solution.py:12
  69.4 6.5 %scatter_fusion.1 = f32[4,512]{0,1:T(8,128)S(1)} fusion(f32[4,512]{0,1:T(8,128)S(1)} %slice.170, s32[1024]{0:T(1024)S(1)} %bitcast.121, f32[1024,4]{1,0:T(8,128)} %bitcast.8), kind=kCustom, calls=%fused_computation.11 | custom fusion | flops 4096 | bytes 53248 | tf_op jit(solution)/shard_map/scatter-add | solution.py:69
  76.0 6.5 %scatter_fusion.2 = f32[4,512]{0,1:T(8,128)S(1)} fusion(f32[4,512]{0,1:T(8,128)S(1)} %scatter_fusion.1, s32[1024]{0:T(1024)S(1)} %bitcast.120, f32[1024,4]{1,0:T(8,128)} %bitcast.12), kind=kCustom, calls=%fused_computation.12 | custom fusion | flops 4096 | bytes 53248 | tf_op jit(solution)/shard_map/scatter-add | solution.py:70
  82.5 6.5 %scatter_fusion.3 = f32[4,512]{0,1:T(8,128)S(1)} fusion(f32[4,512]{0,1:T(8,128)S(1)} %scatter_fusion.2, s32[1024]{0:T(1024)S(1)} %bitcast.119, f32[1024,4]{1,0:T(8,128)} %bitcast.17), kind=kCustom, calls=%fused_computation.13 | custom fusion | flops 4096 | bytes 53248 | tf_op jit(solution)/shard_map/scatter-add | solution.py:71
  89.1 6.7 %scatter_fusion.4 = f32[4,512]{0,1:T(8,128)S(1)} fusion(f32[4,512]{0,1:T(8,128)S(1)} %scatter_fusion.3, s32[1024]{0:T(1024)S(1)} %bitcast.118, f32[1024,4]{1,0:T(8,128)} %bitcast.22), kind=kCustom, calls=%fused_computation.14 | custom fusion | flops 4096 | bytes 53248 | tf_op jit(solution)/shard_map/scatter-add | solution.py:72
  96.1 5.5 %gather_fusion = f32[2048,4]{1,0:T(8,128)S(1)} fusion(f32[4,512]{0,1:T(8,128)S(1)} %copy.112, s32[2048]{0:T(1024)S(1)} %broadcast_clamp_fusion.3), kind=kCustom, calls=%fused_computation | custom fusion | bytes 73728 | tf_op jit(solution)/shard_map/gather | solution.py:37
  102.0 4.7 %collective-permute-start.5 = (f32[4,1,2,512]{3,1,2,0:T(1,128)S(1)}, f32[4,1,2,512]{3,1,2,0:T(1,128)S(1)}, u32[]{:S(2)}, u32[]{:S(2)}) collective-permute-start(f32[4,1,2,512]{3,1,2,0:T(1,128)S(1)} %get-tuple-element.27), channel_id=1, source_target_pairs={{4,0},{8,4},{12,8},{16,12},{20,16},{24,20},{28,24},{0,28},{5,1},{9... | collective-permute-start | bytes 49160 | tf_op jit(solution)/shard_map/ppermute | solution.py:23
  108.6 1.7 collective-permute-start.7
  114.7 26.0 %gather_fusion.1 = f32[7168,4]{1,0:T(8,128)} fusion(f32[4,4608]{0,1:T(8,128)} %constant_dynamic-update-slice_fusion, s32[7168]{0:T(1024)S(1)} %broadcast_clamp_fusion), kind=kCustom, calls=%fused_computation.1 | custom fusion | bytes 258048 | tf_op jit(solution)/shard_map/gather | solution.py:78
  140.6 2.6 copy.113
  143.5 5.5 %gather_fusion.2 = f32[2048,4]{1,0:T(8,128)S(1)} fusion(f32[4,512]{0,1:T(8,128)S(1)} %copy.121, s32[2048]{0:T(1024)S(1)} %broadcast_clamp_fusion.3), kind=kCustom, calls=%fused_computation.2 | custom fusion | bytes 73728 | tf_op jit(solution)/shard_map/gather | solution.py:37
  150.9 3.3 %collective-permute-start.9 = (f32[4,1,2,512]{3,1,2,0:T(1,128)S(1)}, f32[4,1,2,512]{3,1,2,0:T(1,128)S(1)}, u32[]{:S(2)}, u32[]{:S(2)}) collective-permute-start(f32[4,1,2,512]{3,1,2,0:T(1,128)S(1)} %get-tuple-element.25), channel_id=1, source_target_pairs={{4,0},{8,4},{12,8},{16,12},{20,16},{24,20},{28,24},{0,28},{5,1},{9... | collective-permute-start | bytes 49160 | tf_op jit(solution)/shard_map/ppermute | solution.py:23
  162.0 26.0 %gather_fusion.3 = f32[7168,4]{1,0:T(8,128)} fusion(f32[4,4608]{0,1:T(8,128)} %constant_dynamic-update-slice_fusion.5, s32[7168]{0:T(1024)S(1)} %broadcast_clamp_fusion), kind=kCustom, calls=%fused_computation.3 | custom fusion | bytes 258048 | tf_op jit(solution)/shard_map/gather | solution.py:78
  188.0 2.6 copy.122
  190.8 5.5 %gather_fusion.4 = f32[2048,4]{1,0:T(8,128)S(1)} fusion(f32[4,512]{0,1:T(8,128)S(1)} %copy.130, s32[2048]{0:T(1024)S(1)} %broadcast_clamp_fusion.3), kind=kCustom, calls=%fused_computation.4 | custom fusion | bytes 73728 | tf_op jit(solution)/shard_map/gather | solution.py:37
  196.7 4.9 %collective-permute-start.13 = (f32[4,1,2,512]{3,1,2,0:T(1,128)S(1)}, f32[4,1,2,512]{3,1,2,0:T(1,128)S(1)}, u32[]{:S(2)}, u32[]{:S(2)}) collective-permute-start(f32[4,1,2,512]{3,1,2,0:T(1,128)S(1)} %get-tuple-element.23), channel_id=1, source_target_pairs={{4,0},{8,4},{12,8},{16,12},{20,16},{24,20},{28,24},{0,28},{5,1},{9... | collective-permute-start | bytes 49160 | tf_op jit(solution)/shard_map/ppermute | solution.py:23
  209.4 26.0 %gather_fusion.5 = f32[7168,4]{1,0:T(8,128)} fusion(f32[4,4608]{0,1:T(8,128)} %constant_dynamic-update-slice_fusion.10, s32[7168]{0:T(1024)S(1)} %broadcast_clamp_fusion), kind=kCustom, calls=%fused_computation.5 | custom fusion | bytes 258048 | tf_op jit(solution)/shard_map/gather | solution.py:78
  235.4 2.6 copy.131
  238.2 5.5 %gather_fusion.6 = f32[2048,4]{1,0:T(8,128)S(1)} fusion(f32[4,512]{0,1:T(8,128)S(1)} %copy.139, s32[2048]{0:T(1024)S(1)} %broadcast_clamp_fusion.3), kind=kCustom, calls=%fused_computation.6 | custom fusion | bytes 73728 | tf_op jit(solution)/shard_map/gather | solution.py:37
  244.1 4.9 %collective-permute-start.17 = (f32[4,1,2,512]{3,1,2,0:T(1,128)S(1)}, f32[4,1,2,512]{3,1,2,0:T(1,128)S(1)}, u32[]{:S(2)}, u32[]{:S(2)}) collective-permute-start(f32[4,1,2,512]{3,1,2,0:T(1,128)S(1)} %get-tuple-element.21), channel_id=1, source_target_pairs={{4,0},{8,4},{12,8},{16,12},{20,16},{24,20},{28,24},{0,28},{5,1},{9... | collective-permute-start | bytes 49160 | tf_op jit(solution)/shard_map/ppermute | solution.py:23
  249.1 1.6 collective-permute-done.16
  250.9 1.6 collective-permute-start.19
  256.2 9.8 %gather_fusion.8 = f32[3072,4]{1,0:T(8,128)S(1)} fusion(f32[4,4608]{0,1:T(8,128)} %copy-done.2, s32[3072]{0:T(1024)S(1)} %get-tuple-element.31), kind=kCustom, calls=%fused_computation.8 | custom fusion | bytes 110592 | tf_op jit(solution)/shard_map/gather | solution.py:81
  266.0 1.6 slice.202
  267.6 9.8 %gather_fusion.7 = f32[3072,4]{1,0:T(8,128)S(1)} fusion(f32[4,4608]{0,1:T(8,128)} %copy-done.2, s32[3072]{0:T(1024)S(1)} %get-tuple-element.40), kind=kCustom, calls=%fused_computation.7 | custom fusion | bytes 110592 | tf_op jit(solution)/shard_map/gather | solution.py:82
  277.4 1.6 slice.203
  279.6 2.0 copy.140
  (151 shorter events, 35.7 us)
Async XLA Ops:
  0.0 5.6 %copy-start.7 = (s32[3072]{0:T(1024)S(1)}, s32[3072]{0:T(1024)}, u32[]{:S(2)}) copy-start(s32[3072]{0:T(1024)} %param.12) | copy-start | bytes 36868
  0.0 5.6 %copy-start.8 = (s32[3072]{0:T(1024)S(1)}, s32[3072]{0:T(1024)}, u32[]{:S(2)}) copy-start(s32[3072]{0:T(1024)} %param.13) | copy-start | bytes 36868
  41.7 7.9 %copy-start.5 = (s32[2,2,512]{2,1,0:T(2,128)S(1)}, s32[2,2,512]{2,1,0:T(2,128)}, u32[]{:S(2)}) copy-start(s32[2,2,512]{2,1,0:T(2,128)} %param.17) | copy-start | bytes 24580
  41.8 8.1 %copy-start.6 = (s32[14,512]{1,0:T(8,128)S(1)}, s32[14,512]{1,0:T(8,128)}, u32[]{:S(2)}) copy-start(s32[14,512]{1,0:T(8,128)} %param.14) | copy-start | bytes 86020
  41.8 8.1 %copy-start.1 = (bf16[4,14,512]{2,0,1:T(4,128)(2,1)S(1)}, bf16[4,14,512]{2,0,1:T(4,128)(2,1)}, u32[]{:S(2)}) copy-start(bf16[4,14,512]{2,0,1:T(4,128)(2,1)} %param.15) | copy-start | bytes 172036
  41.8 54.2 %copy-start.10 = (f32[4,512]{1,0:T(4,128)S(1)}, f32[4,512]{1,0:T(4,128)}, u32[]{:S(2)}) copy-start(f32[4,512]{1,0:T(4,128)} %param.16) | copy-start | bytes 24580
  43.0 26.4 %collective-permute-start = (f32[4,2,512]{0,2,1:T(8,128)}, f32[4,2,512]{0,2,1:T(8,128)}, u32[]{:S(2)}, u32[]{:S(2)}) collective-permute-start(f32[4,2,512]{0,2,1:T(8,128)} %get-tuple-element.10), channel_id=1, source_target_pairs={{4,0},{8,4},{12,8},{16,12},{20,16},{24,20},{28,24},{0,28},{5,1},{9... | collective-permute-start | bytes 49160 | tf_op jit(solution)/shard_map/ppermute | solution.py:12
  49.0 27.0 %collective-permute-start.1 = (f32[4,2,512]{0,2,1:T(8,128)}, f32[4,2,512]{0,2,1:T(8,128)}, u32[]{:S(2)}, u32[]{:S(2)}) collective-permute-start(f32[4,2,512]{0,2,1:T(8,128)} %get-tuple-element.9), channel_id=1, source_target_pairs={{28,0},{0,4},{4,8},{8,12},{12,16},{16,20},{20,24},{24,28},{29,1},{... | collective-permute-start | bytes 49160 | tf_op jit(solution)/shard_map/ppermute | solution.py:12
  49.0 33.5 %collective-permute-start.2 = (f32[4,2,512]{0,2,1:T(8,128)}, f32[4,2,512]{0,2,1:T(8,128)}, u32[]{:S(2)}, u32[]{:S(2)}) collective-permute-start(f32[4,2,512]{0,2,1:T(8,128)} %get-tuple-element.8), channel_id=1, source_target_pairs={{1,0},{2,1},{3,2},{0,3},{5,4},{6,5},{7,6},{4,7},{9,8},{10,9},{11,1... | collective-permute-start | bytes 49160 | tf_op jit(solution)/shard_map/ppermute | solution.py:12
  49.7 39.4 %collective-permute-start.3 = (f32[4,2,512]{0,2,1:T(8,128)S(1)}, f32[4,2,512]{0,2,1:T(8,128)}, u32[]{:S(2)}, u32[]{:S(2)}) collective-permute-start(f32[4,2,512]{0,2,1:T(8,128)S(1)} %get-tuple-element.7), channel_id=1, source_target_pairs={{3,0},{0,1},{1,2},{2,3},{7,4},{4,5},{5,6},{6,7},{11,8},{8,9},{9,10... | collective-permute-start | bytes 49160 | tf_op jit(solution)/shard_map/ppermute | solution.py:12
  102.0 6.5 %collective-permute-start.4 = (f32[4,1,2,512]{3,1,2,0:T(1,128)S(1)}, f32[4,1,2,512]{3,1,2,0:T(1,128)S(1)}, u32[]{:S(2)}, u32[]{:S(2)}) collective-permute-start(f32[4,1,2,512]{3,1,2,0:T(1,128)S(1)} %get-tuple-element.28), channel_id=1, source_target_pairs={{0,4},{4,8},{8,12},{12,16},{16,20},{20,24},{24,28},{28,0},{1,5},{5... | collective-permute-start | bytes 49160 | tf_op jit(solution)/shard_map/ppermute | solution.py:22
  102.0 6.4 %collective-permute-start.5 = (f32[4,1,2,512]{3,1,2,0:T(1,128)S(1)}, f32[4,1,2,512]{3,1,2,0:T(1,128)S(1)}, u32[]{:S(2)}, u32[]{:S(2)}) collective-permute-start(f32[4,1,2,512]{3,1,2,0:T(1,128)S(1)} %get-tuple-element.27), channel_id=1, source_target_pairs={{4,0},{8,4},{12,8},{16,12},{20,16},{24,20},{28,24},{0,28},{5,1},{9... | collective-permute-start | bytes 49160 | tf_op jit(solution)/shard_map/ppermute | solution.py:23
  108.5 3.9 %collective-permute-start.6 = (f32[4,4,1,512]{3,1,2,0:T(4,128)S(1)}, f32[4,4,1,512]{3,1,2,0:T(4,128)S(1)}, u32[]{:S(2)}, u32[]{:S(2)}) collective-permute-start(f32[4,4,1,512]{3,1,2,0:T(4,128)S(1)} %get-tuple-element.18), channel_id=1, source_target_pairs={{0,1},{1,2},{2,3},{3,0},{4,5},{5,6},{6,7},{7,4},{8,9},{9,10},{10,1... | collective-permute-start | bytes 98312 | tf_op jit(solution)/shard_map/ppermute | solution.py:22
  108.6 4.1 %collective-permute-start.7 = (f32[4,4,1,512]{3,1,2,0:T(4,128)S(1)}, f32[4,4,1,512]{3,1,2,0:T(4,128)S(1)}, u32[]{:S(2)}, u32[]{:S(2)}) collective-permute-start(f32[4,4,1,512]{3,1,2,0:T(4,128)S(1)} %get-tuple-element.17), channel_id=1, source_target_pairs={{1,0},{2,1},{3,2},{0,3},{5,4},{6,5},{7,6},{4,7},{9,8},{10,9},{11,1... | collective-permute-start | bytes 98312 | tf_op jit(solution)/shard_map/ppermute | solution.py:23
  149.3 6.5 %collective-permute-start.8 = (f32[4,1,2,512]{3,1,2,0:T(1,128)S(1)}, f32[4,1,2,512]{3,1,2,0:T(1,128)S(1)}, u32[]{:S(2)}, u32[]{:S(2)}) collective-permute-start(f32[4,1,2,512]{3,1,2,0:T(1,128)S(1)} %get-tuple-element.26), channel_id=1, source_target_pairs={{0,4},{4,8},{8,12},{12,16},{16,20},{20,24},{24,28},{28,0},{1,5},{5... | collective-permute-start | bytes 49160 | tf_op jit(solution)/shard_map/ppermute | solution.py:22
  150.9 5.0 %collective-permute-start.9 = (f32[4,1,2,512]{3,1,2,0:T(1,128)S(1)}, f32[4,1,2,512]{3,1,2,0:T(1,128)S(1)}, u32[]{:S(2)}, u32[]{:S(2)}) collective-permute-start(f32[4,1,2,512]{3,1,2,0:T(1,128)S(1)} %get-tuple-element.25), channel_id=1, source_target_pairs={{4,0},{8,4},{12,8},{16,12},{20,16},{24,20},{28,24},{0,28},{5,1},{9... | collective-permute-start | bytes 49160 | tf_op jit(solution)/shard_map/ppermute | solution.py:23
  155.9 3.9 %collective-permute-start.10 = (f32[4,4,1,512]{3,1,2,0:T(4,128)S(1)}, f32[4,4,1,512]{3,1,2,0:T(4,128)S(1)}, u32[]{:S(2)}, u32[]{:S(2)}) collective-permute-start(f32[4,4,1,512]{3,1,2,0:T(4,128)S(1)} %get-tuple-element.16), channel_id=1, source_target_pairs={{0,1},{1,2},{2,3},{3,0},{4,5},{5,6},{6,7},{7,4},{8,9},{9,10},{10,1... | collective-permute-start | bytes 98312 | tf_op jit(solution)/shard_map/ppermute | solution.py:22
  156.2 3.9 %collective-permute-start.11 = (f32[4,4,1,512]{3,1,2,0:T(4,128)S(1)}, f32[4,4,1,512]{3,1,2,0:T(4,128)S(1)}, u32[]{:S(2)}, u32[]{:S(2)}) collective-permute-start(f32[4,4,1,512]{3,1,2,0:T(4,128)S(1)} %get-tuple-element.15), channel_id=1, source_target_pairs={{1,0},{2,1},{3,2},{0,3},{5,4},{6,5},{7,6},{4,7},{9,8},{10,9},{11,1... | collective-permute-start | bytes 98312 | tf_op jit(solution)/shard_map/ppermute | solution.py:23
  196.6 6.6 %collective-permute-start.12 = (f32[4,1,2,512]{3,1,2,0:T(1,128)S(1)}, f32[4,1,2,512]{3,1,2,0:T(1,128)S(1)}, u32[]{:S(2)}, u32[]{:S(2)}) collective-permute-start(f32[4,1,2,512]{3,1,2,0:T(1,128)S(1)} %get-tuple-element.24), channel_id=1, source_target_pairs={{0,4},{4,8},{8,12},{12,16},{16,20},{20,24},{24,28},{28,0},{1,5},{5... | collective-permute-start | bytes 49160 | tf_op jit(solution)/shard_map/ppermute | solution.py:22
  196.7 6.5 %collective-permute-start.13 = (f32[4,1,2,512]{3,1,2,0:T(1,128)S(1)}, f32[4,1,2,512]{3,1,2,0:T(1,128)S(1)}, u32[]{:S(2)}, u32[]{:S(2)}) collective-permute-start(f32[4,1,2,512]{3,1,2,0:T(1,128)S(1)} %get-tuple-element.23), channel_id=1, source_target_pairs={{4,0},{8,4},{12,8},{16,12},{20,16},{24,20},{28,24},{0,28},{5,1},{9... | collective-permute-start | bytes 49160 | tf_op jit(solution)/shard_map/ppermute | solution.py:23
  203.3 3.9 %collective-permute-start.14 = (f32[4,4,1,512]{3,1,2,0:T(4,128)S(1)}, f32[4,4,1,512]{3,1,2,0:T(4,128)S(1)}, u32[]{:S(2)}, u32[]{:S(2)}) collective-permute-start(f32[4,4,1,512]{3,1,2,0:T(4,128)S(1)} %get-tuple-element.14), channel_id=1, source_target_pairs={{0,1},{1,2},{2,3},{3,0},{4,5},{5,6},{6,7},{7,4},{8,9},{9,10},{10,1... | collective-permute-start | bytes 98312 | tf_op jit(solution)/shard_map/ppermute | solution.py:22
  203.6 3.9 %collective-permute-start.15 = (f32[4,4,1,512]{3,1,2,0:T(4,128)S(1)}, f32[4,4,1,512]{3,1,2,0:T(4,128)S(1)}, u32[]{:S(2)}, u32[]{:S(2)}) collective-permute-start(f32[4,4,1,512]{3,1,2,0:T(4,128)S(1)} %get-tuple-element.13), channel_id=1, source_target_pairs={{1,0},{2,1},{3,2},{0,3},{5,4},{6,5},{7,6},{4,7},{9,8},{10,9},{11,1... | collective-permute-start | bytes 98312 | tf_op jit(solution)/shard_map/ppermute | solution.py:23
  244.1 6.6 %collective-permute-start.16 = (f32[4,1,2,512]{3,1,2,0:T(1,128)S(1)}, f32[4,1,2,512]{3,1,2,0:T(1,128)S(1)}, u32[]{:S(2)}, u32[]{:S(2)}) collective-permute-start(f32[4,1,2,512]{3,1,2,0:T(1,128)S(1)} %get-tuple-element.22), channel_id=1, source_target_pairs={{0,4},{4,8},{8,12},{12,16},{16,20},{20,24},{24,28},{28,0},{1,5},{5... | collective-permute-start | bytes 49160 | tf_op jit(solution)/shard_map/ppermute | solution.py:22
  244.1 6.6 %collective-permute-start.17 = (f32[4,1,2,512]{3,1,2,0:T(1,128)S(1)}, f32[4,1,2,512]{3,1,2,0:T(1,128)S(1)}, u32[]{:S(2)}, u32[]{:S(2)}) collective-permute-start(f32[4,1,2,512]{3,1,2,0:T(1,128)S(1)} %get-tuple-element.21), channel_id=1, source_target_pairs={{4,0},{8,4},{12,8},{16,12},{20,16},{24,20},{28,24},{0,28},{5,1},{9... | collective-permute-start | bytes 49160 | tf_op jit(solution)/shard_map/ppermute | solution.py:23
  250.8 3.4 %collective-permute-start.18 = (f32[4,4,1,512]{3,1,2,0:T(4,128)S(1)}, f32[4,4,1,512]{3,1,2,0:T(4,128)S(1)}, u32[]{:S(2)}, u32[]{:S(2)}) collective-permute-start(f32[4,4,1,512]{3,1,2,0:T(4,128)S(1)} %get-tuple-element.12), channel_id=1, source_target_pairs={{0,1},{1,2},{2,3},{3,0},{4,5},{5,6},{6,7},{7,4},{8,9},{9,10},{10,1... | collective-permute-start | bytes 98312 | tf_op jit(solution)/shard_map/ppermute | solution.py:22
  250.9 3.5 %collective-permute-start.19 = (f32[4,4,1,512]{3,1,2,0:T(4,128)S(1)}, f32[4,4,1,512]{3,1,2,0:T(4,128)S(1)}, u32[]{:S(2)}, u32[]{:S(2)}) collective-permute-start(f32[4,4,1,512]{3,1,2,0:T(4,128)S(1)} %get-tuple-element.11), channel_id=1, source_target_pairs={{1,0},{2,1},{3,2},{0,3},{5,4},{6,5},{7,6},{4,7},{9,8},{10,9},{11,1... | collective-permute-start | bytes 98312 | tf_op jit(solution)/shard_map/ppermute | solution.py:23
  254.8 1.4 copy-start.2
  279.5 2.0 copy-start
  279.5 2.5 copy-start.3
  279.6 2.6 copy-start.4
  279.6 2.6 copy-start.9
where the time goes:
time: 284 us; the launch traced here: 283 us
  local copies, waits for them, and re-layouts  157 us (55%)
  other arithmetic  66.3 us (23%)
  starting transfers between devices  33.4 us (12%)
  waiting for transfers between devices  25 us (9%)
    gather x6, local copies, waits for them, and re-layouts, body(): widened[:, stencil_index]  85.7 us
    scatter-add x2, other arithmetic, body(): edge_terms.at[:, edge_tail].add(vals_tail).at[:, edge_head].add(vals_head)  35.9 us
    ppermute x8, starting transfers between devices, with_halo(): after = lax.ppermute(leading, axis, down)  24.2 us
    gather x8, local copies, waits for them, and re-layouts, ghost_values(): blocks = owned_vals[:, send_index]  23.2 us
    ppermute x4, waiting for transfers between devices, shifted(): return lax.ppermute(block, axis, route)  19.5 us
    unnamed x42, local copies, waits for them, and re-layouts  11.3 us
    gather x1, local copies, waits for them, and re-layouts, body(): at_tail = widened[:, edge_tail]  9.78 us
    gather x1, local copies, waits for them, and re-layouts, body(): at_head = widened[:, edge_head]  9.78 us
  transfers between devices with their start and end apart: 20, of which 6 were waited for; matrix products, arithmetic and copies ran while one was open for 11% of the time, Pallas kernels for 0%

commit v1 on v0

v1 whole, which is shorter than its diff:
```python
import functools

import jax
import jax.numpy as jnp
from jax import lax
from jax.experimental import pallas as pl
from jax.experimental.pallas import tpu as pltpu
from jax.sharding import PartitionSpec as P

SWEEPS = 4
LANES = 128
OPP = (0, 2, 1, 4, 3)
MESH = pl.DeviceIdType.MESH
DNUMS = lax.GatherDimensionNumbers(
    offset_dims=(),
    collapsed_slice_dims=(1,),
    start_index_map=(1,),
    operand_batching_dims=(0,),
    start_indices_batching_dims=(0,),
)
F32 = jnp.float32
BF16 = jnp.bfloat16


def lane_gather(table, lane):
    return lax.gather(
        table,
        lane[..., None],
        DNUMS,
        slice_sizes=(1, 1),
        mode=lax.GatherScatterMode.PROMISE_IN_BOUNDS,
    )


def nt_dot(a, b):
    return lax.dot_general(a, b, (((1,), (1,)), ((), ())), preferred_element_type=F32)


def kernel(
    res_h, tan_h, tail_h, head_h, sidx_h, coef_h, marg_h, send_h,
    out_ref,
    res, tan, tail, head, sidx, coef, marg, own_send,
    got_send, psend, got_p, tab, onehot, spread, onehot2, spread2,
    cf, bsc, diag, hq, hl, sq, sl, tan2,
    local_sem, send_sem, recv_sem,
):
    G, S = lax.axis_size("grp"), lax.axis_size("sub")
    g, s = lax.axis_index("grp"), lax.axis_index("sub")
    gm, gp = lax.rem(g + G - 1, G), lax.rem(g + 1, G)
    sm, sp = lax.rem(s + S - 1, S), lax.rem(s + 1, S)
    peer = (None, (gm, s), (gp, s), (g, sm), (g, sp))
    order = (4, 3, 2, 1)
    nrow = marg.shape[1] // LANES
    erow = res.shape[0]
    stencil = sidx.shape[0]
    vrow = 4 * nrow
    nq = 5 * nrow
    hrow = got_send.shape[3] // LANES

    barrier = pltpu.get_barrier_semaphore()
    for o in order:
        pl.semaphore_signal(barrier, inc=1, device_id=peer[o], device_id_type=MESH)
    pairs = (
        (tail_h, tail), (res_h, res), (tan_h, tan), (head_h, head),
        (coef_h, coef), (marg_h, marg), (sidx_h, sidx),
    )
    local = [
        pltpu.make_async_copy(src, dst, local_sem.at[i]) for i, (src, dst) in enumerate(pairs)
    ]
    for c in local:
        c.start()

    def exchange(rnd, src, dst):
        copies = {}
        for o in order:
            copies[o] = pltpu.make_async_remote_copy(
                src_ref=src(o),
                dst_ref=dst(OPP[o]),
                send_sem=send_sem.at[rnd, o - 1],
                recv_sem=recv_sem.at[rnd, OPP[o] - 1],
                device_id=peer[o],
                device_id_type=MESH,
            )
            copies[o].start()
        return copies

    def arrived(copies, o):
        copies[OPP[o]].wait_recv()

    pl.semaphore_wait(barrier, 4)
    rounds = [exchange(0, lambda o: send_h, lambda o: got_send.at[o - 1])]

    for c in local:
        c.wait()
    riota = lax.broadcasted_iota(jnp.int32, (vrow, LANES), 0)
    kind = riota // nrow
    rpart = riota - kind * nrow
    liota = lax.broadcasted_iota(jnp.int32, (LANES, LANES), 0)

    def terms(t, sign):
        r = res[t : t + 1, :]
        first = jnp.broadcast_to(r if sign > 0 else -r, (vrow, LANES))
        half = 0.5 * r
        val = first
        for c in range(3):
            v = tan[c : c + 1, t * LANES : (t + 1) * LANES] * half
            val = jnp.where(kind == c + 1, v, val)
        hi = val.astype(BF16).astype(F32)
        return hi, val - hi

    def scatter(spread_ref, onehot_ref, lanes_of, rows_of, owners, sign):
        for t in range(erow):
            cols = slice(t * LANES, (t + 1) * LANES)
            onehot_ref[:, cols] = jnp.where(liota == lanes_of(t), 1.0, 0.0).astype(BF16)
            hi, lo = terms(t, sign)
            row = rows_of(t)
            for o in range(owners):
                hit = row == rpart + o * nrow
                for p, v in enumerate((hi, lo)):
                    base = (p * owners + o) * vrow
                    spread_ref[base : base + vrow, cols] = jnp.where(hit, v, 0.0).astype(BF16)
        both = nt_dot(spread_ref[...], onehot_ref[...])
        return both[: owners * vrow] + both[owners * vrow :]

    own_sum = scatter(
        spread, onehot,
        lambda t: tail[t : t + 1, :] & (LANES - 1),
        lambda t: tail[t : t + 1, :] >> 7,
        1, -1,
    )

    cf[...] = jnp.zeros_like(cf)
    for k in range(4):
        for r in range(nrow):
            cols = slice(r * LANES, (r + 1) * LANES)
            c = coef[k, :, cols].astype(F32)
            d = (1.0 + marg[k : k + 1, cols]) * jnp.sum(jnp.abs(c), axis=0, keepdims=True)
            inv = 1.0 / d
            diag[k * nrow + r : k * nrow + r + 1, :] = inv
            cf[k, :stencil, cols] = c * inv
    for c in range(3):
        for t in range(erow):
            tan2[c * erow + t : c * erow + t + 1, :] = tan[c : c + 1, t * LANES : (t + 1) * LANES]
    sq[...] = jnp.zeros_like(sq)
    sq[:stencil, :] = sidx[...]

    for o in order:
        arrived(rounds[0], o)
    halves = (
        None,
        ((1, 0), (1, 1)),
        ((0, 0), (0, 1)),
        ((0, 1), (1, 1)),
        ((0, 0), (1, 0)),
    )

    def compose(x):
        lane = x & (LANES - 1)
        row = x >> 7
        y = x
        at = nrow
        for o in range(1, 5):
            for a, b in halves[o]:
                for r in range(hrow):
                    line = got_send[o - 1, a, b : b + 1, r * LANES : (r + 1) * LANES]
                    line = jnp.broadcast_to(line + o * nrow * LANES, x.shape)
                    y = jnp.where(row == at, lane_gather(line, lane), y)
                    at += 1
        return y

    for i in range(erow // 8):
        y = compose(head[i * 8 : i * 8 + 8, :])
        hq[i * 8 : i * 8 + 8, :] = y >> 7
        hl[i * 8 : i * 8 + 8, :] = y & (LANES - 1)

    parts = scatter(
        spread2, onehot2,
        lambda t: hl[t : t + 1, :],
        lambda t: hq[t : t + 1, :],
        5, 1,
    )
    psend[...] = parts[vrow:]
    own_sum = own_sum + parts[:vrow]
    rounds.append(
        exchange(
            1,
            lambda o: psend.at[pl.ds((o - 1) * vrow, vrow)],
            lambda o: got_p.at[pl.ds((o - 1) * vrow, vrow)],
        )
    )

    srows = sq.shape[0] // 8
    for i in range(srows):
        for r in range(nrow):
            cols = slice(r * LANES, (r + 1) * LANES)
            y = compose(sq[i * 8 : i * 8 + 8, cols])
            sq[i * 8 : i * 8 + 8, cols] = y >> 7
            sl[i * 8 : i * 8 + 8, cols] = y & (LANES - 1)

    for o in order:
        arrived(rounds[1], o)
        own_sum = own_sum + got_p[(o - 1) * vrow : o * vrow, :]
    bsc[...] = own_sum * diag[...]

    def look(rnd, o, r, k, shape):
        at = o * vrow + k * nrow + r
        return jnp.broadcast_to(tab[rnd, at : at + 1, :], shape)

    def add_rows(rnd, o, rows, lanes, accs):
        for r in range(nrow):
            for i in range(len(rows)):
                hit = rows[i] == o * nrow + r
                for k in range(4):
                    v = lane_gather(look(rnd, o, r, k, rows[i].shape), lanes[i])
                    accs[i][k] = v if accs[i][k] is None else jnp.where(hit, v, accs[i][k])

    for rnd in range(SWEEPS):
        if rnd == 0:
            tab[rnd, :vrow, :] = bsc[...]
        copies = exchange(
            2 + rnd,
            lambda o: tab.at[rnd, pl.ds(0, vrow)],
            lambda o: tab.at[rnd, pl.ds(o * vrow, vrow)],
        )
        rounds.append(copies)
        if rnd < SWEEPS - 1:
            where = [(slice(i * 8, i * 8 + 8), slice(r * LANES, (r + 1) * LANES)) for i in range(srows) for r in range(nrow)]
            rows = [sq[w] for w in where]
            lanes = [sl[w] for w in where]
            accs = [[None] * 4 for _ in where]
            add_rows(rnd, 0, rows, lanes, accs)
            for o in order:
                arrived(copies, o)
                add_rows(rnd, o, rows, lanes, accs)
            for k in range(4):
                for r in range(nrow):
                    total = None
                    for i in range(srows):
                        n = i * nrow + r
                        v = accs[n][k] * cf[(k,) + where[n]]
                        total = v if total is None else total + v
                    at = k * nrow + r
                    tab[rnd + 1, at : at + 1, :] = bsc[at : at + 1, :] - jnp.sum(total, axis=0, keepdims=True)

    last = SWEEPS - 1
    n3 = erow // 8
    where = [slice(i * 8, i * 8 + 8) for i in range(n3)]
    tails = [tail[w, :] for w in where]
    tacc = [[None] * 4 for _ in where]
    add_rows(last, 0, [t >> 7 for t in tails], [t & (LANES - 1) for t in tails], tacc)
    rows = [hq[w, :] for w in where]
    lanes = [hl[w, :] for w in where]
    hacc = [[None] * 4 for _ in where]
    add_rows(last, 0, rows, lanes, hacc)
    for o in order:
        arrived(copies, o)
        add_rows(last, o, rows, lanes, hacc)
    for i, w in enumerate(where):
        mixed = None
        for c in range(3):
            v = tan2[c * erow + i * 8 : c * erow + i * 8 + 8, :] * (tacc[i][c + 1] + hacc[i][c + 1])
            mixed = v if mixed is None else mixed + v
        out_ref[w, :] = (hacc[i][0] - tacc[i][0]) + 0.5 * mixed

    for copies in rounds:
        for o in order:
            copies[o].wait_send()


def body(
    residual, edge_scale, tangent, edge_tail, edge_head,
    stencil_index, stencil_coef, diag_margin, send_index,
):
    edges = residual.shape[0]
    erow = edges // LANES
    nodes = diag_margin.shape[1]
    nrow = nodes // LANES
    vrow = 4 * nrow
    stencil = stencil_index.shape[0]
    spad = -(-stencil // 8) * 8
    square = lambda x: x.reshape(erow, LANES)
    anyspace = pl.BlockSpec(memory_space=pl.ANY)
    vm = pltpu.VMEM
    i32 = jnp.int32
    gathered = pl.pallas_call(
        kernel,
        out_shape=jax.ShapeDtypeStruct((erow, LANES), F32),
        in_specs=[anyspace] * 8,
        out_specs=pl.BlockSpec(memory_space=vm),
        scratch_shapes=[
            vm((erow, LANES), F32),
            vm(tangent.shape, F32),
            vm((erow, LANES), i32),
            vm((erow, LANES), i32),
            vm(stencil_index.shape, i32),
            vm(stencil_coef.shape, BF16),
            vm(diag_margin.shape, F32),
            vm(send_index.shape, i32),
            vm((4,) + send_index.shape, i32),
            vm((4 * vrow, LANES), F32),
            vm((4 * vrow, LANES), F32),
            vm((SWEEPS, 5 * vrow, LANES), F32),
            vm((LANES, edges), BF16),
            vm((2 * vrow, edges), BF16),
            vm((LANES, edges), BF16),
            vm((10 * vrow, edges), BF16),
            vm((4, spad, nodes), F32),
            vm((vrow, LANES), F32),
            vm((vrow, LANES), F32),
            vm((erow, LANES), i32),
            vm((erow, LANES), i32),
            vm((spad, nodes), i32),
            vm((spad, nodes), i32),
            vm((3 * erow, LANES), F32),
            pltpu.SemaphoreType.DMA((7,)),
            pltpu.SemaphoreType.DMA((SWEEPS + 2, 4)),
            pltpu.SemaphoreType.DMA((SWEEPS + 2, 4)),
        ],
        compiler_params=pltpu.CompilerParams(collective_id=0, has_side_effects=True),
    )(
        square(residual), tangent, square(edge_tail), square(edge_head),
        stencil_index, stencil_coef, diag_margin, send_index,
    )
    return edge_scale * residual + gathered.reshape(edges)


def solution(mesh):
    return jax.shard_map(
        body,
        mesh=mesh,
        in_specs=(
            P(("grp", "sub")),
            P(("grp", "sub")),
            P(None, ("grp", "sub")),
            P(("grp", "sub")),
            P(("grp", "sub")),
            P(None, ("grp", "sub")),
            P(None, None, ("grp", "sub")),
            P(None, ("grp", "sub")),
            P("grp", "sub", None),
        ),
        out_specs=P(("grp", "sub")),
        check_vma=False,
    )
```

time: 284 us -> 37.1 us (0.13)
  local copies, waits for them, and re-layouts: 157 us -> 1.45 us
  other arithmetic: 66.3 us -> 1.31 us
  Pallas kernels: 0 us -> 34.1 us
  starting transfers between devices: 33.4 us -> 0 us
  waiting for transfers between devices: 25 us -> 0 us
    gather x16 -> x0, local copies, waits for them, and re-layouts: 128 us -> none  [the longest x6 85.7 us: body(): widened[:, stencil_index]]
    scatter-add x6 -> x0, other arithmetic: 62.3 us -> none  [the longest x2 35.9 us: body(): edge_terms.at[:, edge_tail].add(vals_tail).at[:, edge_head].add(vals_head)]
    pallas_call x0 -> x1, Pallas kernels: none -> 34.1 us  [body(): pl.pallas_call(kernel, out_shape=jax.ShapeDtypeStruct((erow, LANES), F32)...]
    ppermute x20 -> x0, starting transfers between devices: 33.4 us -> none  [the longest x8 24.2 us: with_halo(): after = lax.ppermute(leading, axis, down)]
    ppermute x20 -> x0, waiting for transfers between devices: 25 us -> none  [the longest x4 19.5 us: shifted(): return lax.ppermute(block, axis, route)]
    unnamed x42 -> x5, local copies, waits for them, and re-layouts: 11.3 us -> 1.45 us
    slice x31 -> x0, local copies, waits for them, and re-layouts: 7.9 us -> none  [the longest x2 3.6 us: body(): at_tail[1:] + at_head[1:]]
    concatenate x6 -> x0, local copies, waits for them, and re-layouts: 5.88 us -> none  [the longest x4 2.55 us: ghost_values(): return jnp.concatenate([owned_vals] + flat_pieces, axis=1)]
  transfers between devices with their start and end apart: 20 -> 0, of which waited for: 6 -> 0; matrix products, arithmetic and copies ran while one was open for 11% -> 0% of each run, Pallas kernels for 0% -> 0%
where the time goes in v1:
time: 37.1 us; the launch traced here: 36.9 us
  Pallas kernels  34.1 us (92%)
  local copies, waits for them, and re-layouts  1.45 us (4%)
  other arithmetic  1.31 us (4%)
    pallas_call x1, Pallas kernels, body(): pl.pallas_call(kernel, out_shape=jax.ShapeDtypeStruct((erow, LANES), F32)...  34.1 us
    unnamed x5, local copies, waits for them, and re-layouts  1.45 us
    add x1, other arithmetic, body(): return edge_scale * residual + gathered.reshape(edges)  1.31 us

profile of v1, /device:TPU:0, one launch (start us, length us, event | category | flops | bytes accessed | tf_op | source)
XLA Modules:
  0.0 36.9 jit_solution(5379649099900239794)
XLA Ops:
  0.0 1.4 %copy.10.coef_h = bf16[4,14,512]{2,1,0:T(8,128)(2,1)} copy(bf16[4,14,512]{2,0,1:T(4,128)(2,1)} %param.15) | data formatting | bytes 114688 | tf_op args[6]
  1.4 0.0 copy-start
  1.4 0.0 copy-start.1
  1.4 34.1 %shard_map.91 = f32[24,128]{1,0:T(8,128)} custom-call(f32[24,128]{1,0:T(8,128)} %bitcast.5, f32[3,3072]{1,0:T(4,128)} %tan_h.1, s32[24,128]{1,0:T(8,128)} %bitcast.6, s32[24,128]{1,0:T(8,128)} %bitcast.7, s32[14,512]{1,0:T(8,128)} %sidx_h.1, bf16[4,14,512]{2,1,0:T(8,128)(2,1)} %copy.10.coef_h, f32[4,512]{1,0:T(4,128)} %marg_h.1, s32[2,2,512]{2,1,0:T(2,128)} %send_h.1), custom_call_target="tpu_custom_call" | custom-call | tf_op jit(solution)/shard_map/pallas_call | solution.py:285
  35.5 0.0 copy-done
  35.5 0.0 copy-done.1
  35.6 1.3 %bitcast_add_fusion = f32[3072]{0:T(1024)} fusion(f32[24,128]{1,0:T(8,128)} %shard_map.91, f32[3072]{0:T(1024)S(1)} %copy-done.1, f32[3072]{0:T(1024)S(1)} %copy-done), kind=kLoop, calls=%fused_computation | loop fusion | flops 6144 | bytes 49152 | tf_op jit(solution)/shard_map/add | solution.py:324
Async XLA Ops:
  1.4 34.1 %copy-start = (f32[3072]{0:T(1024)S(1)}, f32[3072]{0:T(1024)}, u32[]{:S(2)}) copy-start(f32[3072]{0:T(1024)} %param.9) | copy-start | bytes 36868
  1.4 34.1 %copy-start.1 = (f32[3072]{0:T(1024)S(1)}, f32[3072]{0:T(1024)}, u32[]{:S(2)}) copy-start(f32[3072]{0:T(1024)} %param.10) | copy-start | bytes 36868

commit v2 on v1

--- a/solution.py
+++ b/solution.py
@@ -40,7 +40,7 @@
     res_h, tan_h, tail_h, head_h, sidx_h, coef_h, marg_h, send_h,
     out_ref,
     res, tan, tail, head, sidx, coef, marg, own_send,
-    got_send, psend, got_p, tab, onehot, spread, onehot2, spread2,
+    got_send, psend, got_p, tab, onehot, spread, onehot2, spread2, onehot3, spread3, tsum,
     cf, bsc, diag, hq, hl, sq, sl, tan2,
     local_sem, send_sem, recv_sem,
 ):
@@ -62,7 +62,7 @@
         pl.semaphore_signal(barrier, inc=1, device_id=peer[o], device_id_type=MESH)
     pairs = (
         (tail_h, tail), (res_h, res), (tan_h, tan), (head_h, head),
-        (coef_h, coef), (marg_h, marg), (sidx_h, sidx),
+        (send_h, own_send), (coef_h, coef), (marg_h, marg), (sidx_h, sidx),
     )
     local = [
         pltpu.make_async_copy(src, dst, local_sem.at[i]) for i, (src, dst) in enumerate(pairs)
@@ -87,9 +87,6 @@
     def arrived(copies, o):
         copies[OPP[o]].wait_recv()
 
-    pl.semaphore_wait(barrier, 4)
-    rounds = [exchange(0, lambda o: send_h, lambda o: got_send.at[o - 1])]
-
     for c in local:
         c.wait()
     riota = lax.broadcasted_iota(jnp.int32, (vrow, LANES), 0)
@@ -129,11 +126,30 @@
         1, -1,
     )
 
+    parts = scatter(
+        spread2, onehot2,
+        lambda t: head[t : t + 1, :] & (LANES - 1),
+        lambda t: head[t : t + 1, :] >> 7,
+        (nrow + 8 * hrow) // nrow, 1,
+    )
+    psend[...] = parts[vrow:]
+    own_sum = own_sum + parts[:vrow]
+    sent = 2 * 4 * hrow
+
+    lists = tuple((a, b, r) for a in range(2) for b in range(2) for r in range(hrow))
+
+    def own_list(a, b, r):
+        return own_send[a, b : b + 1, r * LANES : (r + 1) * LANES]
+
+    for n, abr in enumerate(lists):
+        hit = liota == (own_list(*abr) & (LANES - 1))
+        onehot3[:, n * LANES : (n + 1) * LANES] = jnp.where(hit, 1.0, 0.0).astype(BF16)
+
     cf[...] = jnp.zeros_like(cf)
     for k in range(4):
         for r in range(nrow):
             cols = slice(r * LANES, (r + 1) * LANES)
-            c = coef[k, :, cols].astype(F32)
+            c = coef[:, k, cols].astype(F32)
             d = (1.0 + marg[k : k + 1, cols]) * jnp.sum(jnp.abs(c), axis=0, keepdims=True)
             inv = 1.0 / d
             diag[k * nrow + r : k * nrow + r + 1, :] = inv
@@ -144,8 +160,41 @@
     sq[...] = jnp.zeros_like(sq)
     sq[:stencil, :] = sidx[...]
 
+    pl.semaphore_wait(barrier, 4)
+    rounds = [
+        exchange(
+            1,
+            lambda o: psend.at[pl.ds((o - 1) * sent, sent)],
+            lambda o: got_p.at[pl.ds((o - 1) * sent, sent)],
+        )
+    ]
+    rounds.append(exchange(0, lambda o: own_send, lambda o: got_send.at[o - 1]))
+
     for o in order:
         arrived(rounds[0], o)
+    block = 4 * hrow
+    for a in range(2):
+        for b in range(2):
+            first = a * sent + b * block
+            second = (2 + b) * sent + a * block
+            at = (a * 2 + b) * block
+            tsum[at : at + block, :] = got_p[first : first + block, :] + got_p[second : second + block, :]
+    for n, (a, b, r) in enumerate(lists):
+        base = (a * 2 + b) * block + r
+        val = jnp.broadcast_to(tsum[base : base + 1, :], (vrow, LANES))
+        for k in range(1, 4):
+            at = base + k * hrow
+            val = jnp.where(kind == k, tsum[at : at + 1, :], val)
+        hit = (own_list(a, b, r) >> 7) == rpart
+        val = jnp.where(hit, val, 0.0)
+        hi = val.astype(BF16)
+        cols = slice(n * LANES, (n + 1) * LANES)
+        spread3[:vrow, cols] = hi
+        spread3[vrow:, cols] = (val - hi.astype(F32)).astype(BF16)
+    back = nt_dot(spread3[...], onehot3[...])
+    own_sum = own_sum + (back[:vrow] + back[vrow:])
+    bsc[...] = own_sum * diag[...]
+
     halves = (
         None,
         ((1, 0), (1, 1)),
@@ -168,39 +217,23 @@
                     at += 1
         return y
 
-    for i in range(erow // 8):
-        y = compose(head[i * 8 : i * 8 + 8, :])
-        hq[i * 8 : i * 8 + 8, :] = y >> 7
-        hl[i * 8 : i * 8 + 8, :] = y & (LANES - 1)
-
-    parts = scatter(
-        spread2, onehot2,
-        lambda t: hl[t : t + 1, :],
-        lambda t: hq[t : t + 1, :],
-        5, 1,
-    )
-    psend[...] = parts[vrow:]
-    own_sum = own_sum + parts[:vrow]
-    rounds.append(
-        exchange(
-            1,
-            lambda o: psend.at[pl.ds((o - 1) * vrow, vrow)],
-            lambda o: got_p.at[pl.ds((o - 1) * vrow, vrow)],
-        )
-    )
+    def compose_all():
+        for o in order:
+            arrived(rounds[1], o)
+        for i in range(srows):
+            for r in range(nrow):
+                cols = slice(r * LANES, (r + 1) * LANES)
+                y = compose(sq[i * 8 : i * 8 + 8, cols])
+                sq[i * 8 : i * 8 + 8, cols] = y >> 7
+                sl[i * 8 : i * 8 + 8, cols] = y & (LANES - 1)
+
+    def compose_heads():
+        for i in range(erow // 8):
+            y = compose(head[i * 8 : i * 8 + 8, :])
+            hq[i * 8 : i * 8 + 8, :] = y >> 7
+            hl[i * 8 : i * 8 + 8, :] = y & (LANES - 1)
 
     srows = sq.shape[0] // 8
-    for i in range(srows):
-        for r in range(nrow):
-            cols = slice(r * LANES, (r + 1) * LANES)
-            y = compose(sq[i * 8 : i * 8 + 8, cols])
-            sq[i * 8 : i * 8 + 8, cols] = y >> 7
-            sl[i * 8 : i * 8 + 8, cols] = y & (LANES - 1)
-
-    for o in order:
-        arrived(rounds[1], o)
-        own_sum = own_sum + got_p[(o - 1) * vrow : o * vrow, :]
-    bsc[...] = own_sum * diag[...]
 
     def look(rnd, o, r, k, shape):
         at = o * vrow + k * nrow + r
@@ -223,6 +256,10 @@
             lambda o: tab.at[rnd, pl.ds(o * vrow, vrow)],
         )
         rounds.append(copies)
+        if rnd == 0:
+            compose_all()
+        if rnd == 1:
+            compose_heads()
         if rnd < SWEEPS - 1:
             where = [(slice(i * 8, i * 8 + 8), slice(r * LANES, (r + 1) * LANES)) for i in range(srows) for r in range(nrow)]
             rows = [sq[w] for w in where]
@@ -278,6 +315,9 @@
     vrow = 4 * nrow
     stencil = stencil_index.shape[0]
     spad = -(-stencil // 8) * 8
+    hrow = send_index.shape[2] // LANES
+    blocks = (nrow + 8 * hrow) // nrow
+    coef = jnp.transpose(stencil_coef, (1, 0, 2))
     square = lambda x: x.reshape(erow, LANES)
     anyspace = pl.BlockSpec(memory_space=pl.ANY)
     vm = pltpu.VMEM
@@ -293,17 +333,20 @@
             vm((erow, LANES), i32),
             vm((erow, LANES), i32),
             vm(stencil_index.shape, i32),
-            vm(stencil_coef.shape, BF16),
+            vm(coef.shape, BF16),
             vm(diag_margin.shape, F32),
             vm(send_index.shape, i32),
             vm((4,) + send_index.shape, i32),
-            vm((4 * vrow, LANES), F32),
-            vm((4 * vrow, LANES), F32),
+            vm((32 * hrow, LANES), F32),
+            vm((32 * hrow, LANES), F32),
             vm((SWEEPS, 5 * vrow, LANES), F32),
             vm((LANES, edges), BF16),
             vm((2 * vrow, edges), BF16),
             vm((LANES, edges), BF16),
-            vm((10 * vrow, edges), BF16),
+            vm((2 * blocks * vrow, edges), BF16),
+            vm((LANES, 4 * send_index.shape[2]), BF16),
+            vm((2 * vrow, 4 * send_index.shape[2]), BF16),
+            vm((16 * hrow, LANES), F32),
             vm((4, spad, nodes), F32),
             vm((vrow, LANES), F32),
             vm((vrow, LANES), F32),
@@ -312,14 +355,14 @@
             vm((spad, nodes), i32),
             vm((spad, nodes), i32),
             vm((3 * erow, LANES), F32),
-            pltpu.SemaphoreType.DMA((7,)),
+            pltpu.SemaphoreType.DMA((8,)),
             pltpu.SemaphoreType.DMA((SWEEPS + 2, 4)),
             pltpu.SemaphoreType.DMA((SWEEPS + 2, 4)),
         ],
         compiler_params=pltpu.CompilerParams(collective_id=0, has_side_effects=True),
     )(
         square(residual), tangent, square(edge_tail), square(edge_head),
-        stencil_index, stencil_coef, diag_margin, send_index,
+        stencil_index, coef, diag_margin, send_index,
     )
     return edge_scale * residual + gathered.reshape(edges)
 

time: 37.1 us -> 31.5 us (0.85)
  Pallas kernels: 34.1 us -> 30 us
  local copies, waits for them, and re-layouts: 1.45 us -> 0.01 us
    pallas_call x1, Pallas kernels: 34.1 us -> 30 us  [body(): pl.pallas_call(kernel, out_shape=jax.ShapeDtypeStruct((erow, LANES), F32)...]
    unnamed x5 -> x4, local copies, waits for them, and re-layouts: 1.45 us -> 0.01 us
where the time goes in v2:
time: 31.5 us; the launch traced here: 31.3 us
  Pallas kernels  30 us (95%)
  other arithmetic  1.31 us (4%)
    pallas_call x1, Pallas kernels, body(): pl.pallas_call(kernel, out_shape=jax.ShapeDtypeStruct((erow, LANES), F32)...  30 us
    add x1, other arithmetic, body(): return edge_scale * residual + gathered.reshape(edges)  1.31 us

profile of v2, /device:TPU:0, one launch (start us, length us, event | category | flops | bytes accessed | tf_op | source)
XLA Modules:
  0.0 31.3 jit_solution(14655948487341481293)
XLA Ops:
  0.0 0.0 copy-start
  0.0 0.0 copy-start.1
  0.0 30.0 %shard_map.91 = f32[24,128]{1,0:T(8,128)} custom-call(f32[24,128]{1,0:T(8,128)} %bitcast.7, f32[3,3072]{1,0:T(4,128)} %tan_h.1, s32[24,128]{1,0:T(8,128)} %bitcast.8, s32[24,128]{1,0:T(8,128)} %bitcast.9, s32[14,512]{1,0:T(8,128)} %sidx_h.1, bf16[14,4,512]{2,1,0:T(4,128)(2,1)} %bitcast.6, f32[4,512]{1,0:T(4,128)} %marg_h.1, s32[2,2,512]{2,1,0:T(2,128)} %send_h.1), custom_call_target="tpu_custom_call" | custom-call | tf_op jit(solution)/shard_map/pallas_call | solution.py:325
  30.0 0.0 copy-done
  30.0 0.0 copy-done.1
  30.0 1.3 %bitcast_add_fusion = f32[3072]{0:T(1024)} fusion(f32[24,128]{1,0:T(8,128)} %shard_map.91, f32[3072]{0:T(1024)S(1)} %copy-done.1, f32[3072]{0:T(1024)S(1)} %copy-done), kind=kLoop, calls=%fused_computation | loop fusion | flops 6144 | bytes 49152 | tf_op jit(solution)/shard_map/add | solution.py:367
Async XLA Ops:
  0.0 30.0 %copy-start = (f32[3072]{0:T(1024)S(1)}, f32[3072]{0:T(1024)}, u32[]{:S(2)}) copy-start(f32[3072]{0:T(1024)} %param.9) | copy-start | bytes 36868
  0.0 30.0 %copy-start.1 = (f32[3072]{0:T(1024)S(1)}, f32[3072]{0:T(1024)}, u32[]{:S(2)}) copy-start(f32[3072]{0:T(1024)} %param.10) | copy-start | bytes 36868

commit v3 on v2

--- a/solution.py
+++ b/solution.py
@@ -86,6 +86,19 @@
 
     def arrived(copies, o):
         copies[OPP[o]].wait_recv()
+
+    near = 2 - lax.rem(g, 2)
+    walk = (4, 3, near, 3 - near)
+
+    def table_here(rnd, o):
+        pltpu.make_async_remote_copy(
+            src_ref=tab.at[rnd, pl.ds(0, vrow)],
+            dst_ref=tab.at[rnd, pl.ds(o * vrow, vrow)],
+            send_sem=send_sem.at[2 + rnd, 0],
+            recv_sem=recv_sem.at[2 + rnd, o - 1],
+            device_id=peer[4],
+            device_id_type=MESH,
+        ).wait_recv()
 
     for c in local:
         c.wait()
@@ -237,7 +250,7 @@
 
     def look(rnd, o, r, k, shape):
         at = o * vrow + k * nrow + r
-        return jnp.broadcast_to(tab[rnd, at : at + 1, :], shape)
+        return jnp.broadcast_to(tab[rnd, pl.ds(at, 1), :], shape)
 
     def add_rows(rnd, o, rows, lanes, accs):
         for r in range(nrow):
@@ -246,6 +259,21 @@
                 for k in range(4):
                     v = lane_gather(look(rnd, o, r, k, rows[i].shape), lanes[i])
                     accs[i][k] = v if accs[i][k] is None else jnp.where(hit, v, accs[i][k])
+
+    sub8 = lax.broadcasted_iota(jnp.int32, (8, LANES), 0)
+
+    def fold(vecs):
+        step = len(vecs) // 2
+        while step:
+            keep = (sub8 & step) == 0
+            vecs = [
+                jnp.where(keep, x, y) + pltpu.roll(jnp.where(keep, y, x), step, axis=0)
+                if step == 4 else
+                jnp.where(keep, x + pltpu.roll(x, 8 - step, axis=0), y + pltpu.roll(y, step, axis=0))
+                for x, y in zip(vecs[:step], vecs[step:])
+            ]
+            step //= 2
+        return vecs[0]
 
     for rnd in range(SWEEPS):
         if rnd == 0:
@@ -266,9 +294,10 @@
             lanes = [sl[w] for w in where]
             accs = [[None] * 4 for _ in where]
             add_rows(rnd, 0, rows, lanes, accs)
-            for o in order:
-                arrived(copies, o)
+            for o in walk:
+                table_here(rnd, o)
                 add_rows(rnd, o, rows, lanes, accs)
+            totals = []
             for k in range(4):
                 for r in range(nrow):
                     total = None
@@ -276,8 +305,9 @@
                         n = i * nrow + r
                         v = accs[n][k] * cf[(k,) + where[n]]
                         total = v if total is None else total + v
-                    at = k * nrow + r
-                    tab[rnd + 1, at : at + 1, :] = bsc[at : at + 1, :] - jnp.sum(total, axis=0, keepdims=True)
+                    totals.append(total)
+            for at in range(0, vrow, 8):
+                tab[rnd + 1, at : at + 8, :] = bsc[at : at + 8, :] - fold(totals[at : at + 8])
 
     last = SWEEPS - 1
     n3 = erow // 8
@@ -289,8 +319,8 @@
     lanes = [hl[w, :] for w in where]
     hacc = [[None] * 4 for _ in where]
     add_rows(last, 0, rows, lanes, hacc)
-    for o in order:
-        arrived(copies, o)
+    for o in walk:
+        table_here(last, o)
         add_rows(last, o, rows, lanes, hacc)
     for i, w in enumerate(where):
         mixed = None

time: 31.5 us -> 30.9 us (0.981)
  Pallas kernels: 30 us -> 29.4 us
    pallas_call x1, Pallas kernels: 30 us -> 29.4 us  [body(): pl.pallas_call(kernel, out_shape=jax.ShapeDtypeStruct((erow, LANES), F32)...]
where the time goes in v3:
time: 30.9 us; the launch traced here: 30.7 us
  Pallas kernels  29.4 us (95%)
  other arithmetic  1.31 us (4%)
    pallas_call x1, Pallas kernels, body(): pl.pallas_call(kernel, out_shape=jax.ShapeDtypeStruct((erow, LANES), F32)...  29.4 us
    add x1, other arithmetic, body(): return edge_scale * residual + gathered.reshape(edges)  1.31 us

profile of v3, /device:TPU:0, one launch (start us, length us, event | category | flops | bytes accessed | tf_op | source)
XLA Modules:
  0.0 30.7 jit_solution(6354892567285792682)
XLA Ops:
  0.0 0.0 copy-start
  0.0 0.0 copy-start.1
  0.0 29.4 %shard_map.91 = f32[24,128]{1,0:T(8,128)} custom-call(f32[24,128]{1,0:T(8,128)} %bitcast.7, f32[3,3072]{1,0:T(4,128)} %tan_h.1, s32[24,128]{1,0:T(8,128)} %bitcast.8, s32[24,128]{1,0:T(8,128)} %bitcast.9, s32[14,512]{1,0:T(8,128)} %sidx_h.1, bf16[14,4,512]{2,1,0:T(4,128)(2,1)} %bitcast.6, f32[4,512]{1,0:T(4,128)} %marg_h.1, s32[2,2,512]{2,1,0:T(2,128)} %send_h.1), custom_call_target="tpu_custom_call" | custom-call | tf_op jit(solution)/shard_map/pallas_call | solution.py:355
  29.4 0.0 copy-done
  29.4 0.0 copy-done.1
  29.4 1.3 %bitcast_add_fusion = f32[3072]{0:T(1024)} fusion(f32[24,128]{1,0:T(8,128)} %shard_map.91, f32[3072]{0:T(1024)S(1)} %copy-done.1, f32[3072]{0:T(1024)S(1)} %copy-done), kind=kLoop, calls=%fused_computation | loop fusion | flops 6144 | bytes 49152 | tf_op jit(solution)/shard_map/add | solution.py:397
Async XLA Ops:
  0.0 29.4 %copy-start = (f32[3072]{0:T(1024)S(1)}, f32[3072]{0:T(1024)}, u32[]{:S(2)}) copy-start(f32[3072]{0:T(1024)} %param.9) | copy-start | bytes 36868
  0.0 29.4 %copy-start.1 = (f32[3072]{0:T(1024)S(1)}, f32[3072]{0:T(1024)}, u32[]{:S(2)}) copy-start(f32[3072]{0:T(1024)} %param.10) | copy-start | bytes 36868
